TPU v7x, 32 devices: a whole 2x2x4 slice. The times are simulated.
32 devices in a mesh: row: 8 (over z, y), col: 4 (over x, core).
Axes of the slice: x: 2, y: 2, z: 4, core: 2. Of those that a mesh axis runs over, the one named last changes fastest.
Arguments:
- densities: bfloat16 [4608, 3072], P(('row', 'col')), may hold values from -0.796875 to 0.796875
- counts: int32 [512], P(('row', 'col')), may hold values from 3 to 9
- coulomb: float32 [3072], replicated, may hold values from 0.05 to 1
- energies: float32 [4608], P(('row', 'col')), may hold values from 8 to 64
- vectors: bfloat16 [4608, 64], P(('row', 'col')), may hold values from -0.09375 to 0.09375
Outputs:
- kernel: float32 [4608, 4608], P('row', 'col')
- product: float32 [4608, 64], P(('row', 'col'))
All inputs are finite; a program needn't handle non-finite values.
Results may differ from a plain program's by a relative error of at most 0.0095.
Values may be sent and summed in bfloat16 or wider, within the bound.
A program may use at most 128 MiB of HBM per device.

v0:
```python
import jax
import jax.numpy as jnp
from jax import lax
from jax.sharding import PartitionSpec as P

SLOT = 9


def body(densities, counts, coulomb, energies, vectors):
    kpoints = counts.shape[0]
    slot_index = lax.broadcasted_iota(jnp.int32, (kpoints, SLOT), 1)
    usable = (slot_index < counts[:, None]).reshape(kpoints * SLOT)
    masked = jnp.where(usable[:, None], densities, jnp.zeros_like(densities))
    weighted = (masked.astype(jnp.float32) * coulomb[None, :]).astype(jnp.bfloat16)
    row_block = lax.all_gather(weighted, "col", axis=0, tiled=True)
    kernel = lax.dot_general(
        row_block,
        lax.all_gather(masked, "row", axis=0, tiled=True),
        (((1,), (1,)), ((), ())),
        preferred_element_type=jnp.float32,
    )
    local_terms = lax.dot_general(
        masked, vectors, (((0,), (0,)), ((), ())), preferred_element_type=jnp.float32
    )
    projected = lax.psum(local_terms, ("row", "col"))
    coupled = jnp.dot(
        weighted.astype(jnp.float32),
        projected,
        precision=lax.Precision.HIGHEST,
        preferred_element_type=jnp.float32,
    )
    diagonal = jnp.where(usable, energies, jnp.zeros_like(energies))
    product = coupled + diagonal[:, None] * vectors.astype(jnp.float32)
    return (kernel, product)


def solution(mesh):
    return jax.shard_map(
        body,
        mesh=mesh,
        in_specs=(
            P(("row", "col"), None),
            P(("row", "col")),
            P(),
            P(("row", "col")),
            P(("row", "col"), None),
        ),
        out_specs=(P("row", "col"), P(("row", "col"), None)),
        check_vma=False,
    )
```

profile of v0, /device:TPU:0, one launch (start us, length us, event | category | flops | bytes accessed | tf_op | source)
XLA Modules:
  0.0 254.9 jit_solution(2723518301834246498)
XLA Ops:
  8.0 0.0 copy-start.2
  8.0 0.0 all-reduce.2.cloned.1.call-start
  8.1 0.7 iota_compare_fusion
  8.8 0.1 lt.18
  8.9 2.5 multiply_convert_fusion
  11.4 0.0 copy-start
  11.4 0.0 copy-done.2
  11.4 0.0 copy-start.3
  11.4 0.0 copy-start.1
  11.4 1.8 fusion.1
  13.2 0.0 all-reduce.2.cloned.1.call-update
  13.2 0.0 all-gather.3.cloned.1.call-start
  13.3 0.5 all-gather.3.cloned.1.call-update
  13.8 0.0 all-gather.5.cloned.1.call-start
  13.9 0.0 copy-done
  13.9 0.5 all-gather.5.cloned.1.call-update
  14.4 0.0 copy-done.3
  14.4 219.2 %all-reduce.2.cloned.1.call-done = f32[3072,64]{1,0:T(8,128)} async-done(((f32[3072,64]{1,0:T(8,128)}), f32[3072,64]{1,0:T(8,128)}) %all-reduce.2.cloned.1.call-update) | async-done | bytes 786448 | tf_op jit(solution)/shard_map/psum | solution.py:25
  233.7 0.0 copy-done.1
  233.7 3.5 %convolution_add_fusion = f32[144,64]{0,1:T(8,128)} fusion(bf16[144,3072]{1,0:T(8,128)(2,1)S(1)} %copy-done.1, f32[3072,64]{1,0:T(8,128)} %all-reduce.2.cloned.1.call-done, bf16[144,64]{0,1:T(8,128)(2,1)S(1)} %copy-done.2, f32[144]{0:T(256)S(1)} %broadcast_select_fusion.1), kind=kOutput, calls=%fused_computation.1 | convolution fusion | flops 339766272 | bytes 1727040 | tf_op jit(solution)/shard_map/dot_general | solution.py:26
  237.1 0.0 all-gather.3.cloned.1.call-done
  237.1 0.0 all-gather.5.cloned.1.call-done
  237.1 10.4 %fusion = f32[576,1152]{1,0:T(8,128)} fusion(bf16[576,3072]{1,0:T(8,128)(2,1)} %all-gather.3.cloned.1.call-done, bf16[1152,3072]{1,0:T(8,128)(2,1)} %all-gather.5.cloned.1.call-done), kind=kOutput, calls=%fused_computation.5 | convolution fusion | flops 4076863488 | bytes 13271040 | tf_op jit(solution)/shard_map/dot_general | solution.py:16
  (1 shorter events, 0.0 us)
Async XLA Ops:
  8.0 3.4 %copy-start.2 = (bf16[144,64]{0,1:T(8,128)(2,1)S(1)}, bf16[144,64]{0,1:T(8,128)(2,1)}, u32[]{:S(2)}) copy-start(bf16[144,64]{0,1:T(8,128)(2,1)} %param.9) | copy-start | bytes 55300
  8.0 225.6 %all-reduce.2.cloned.1.call-start = ((), (), s32[]{:S(2)}) async-start(), calls=%async_computation.2 | async-start | bytes 3145728 | tf_op jit(solution)/shard_map/psum | solution.py:25
  11.4 2.5 copy-start
  11.4 3.0 %copy-start.3 = (f32[144]{0:T(256)S(1)}, f32[144]{0:T(256)}, u32[]{:S(2)}) copy-start(f32[144]{0:T(256)} %param.8) | copy-start | bytes 1732
  11.4 222.2 %copy-start.1 = (bf16[144,3072]{1,0:T(8,128)(2,1)S(1)}, bf16[144,3072]{1,0:T(8,128)(2,1)}, u32[]{:S(2)}) copy-start(bf16[144,3072]{1,0:T(8,128)(2,1)} %get-tuple-element.2) | copy-start | bytes 2654212
  13.2 223.9 %all-gather.3.cloned.1.call-start = ((), (), s32[]{:S(2)}) async-start(), calls=%async_computation | async-start | bytes 4423680 | tf_op jit(solution)/shard_map/all_gather | solution.py:15
  13.8 223.3 %all-gather.5.cloned.1.call-start = ((), (), s32[]{:S(2)}) async-start(), calls=%async_computation.1 | async-start | bytes 7962624 | tf_op jit(solution)/shard_map/all_gather | solution.py:18
Sparse Core Ops, SparseCore 0:
  14.7 218.9 all-reduce.1
Sparse Core Ops, SparseCore 1:
  15.3 34.0 all-gather.2
  51.4 109.7 all-gather.4
where the time goes:
time: 255 us
  waiting for transfers between devices  220 us (86%)
  matrix products  15.6 us (6%)
  between operations  15.5 us (6%)
  other arithmetic  3.27 us (1%)
    psum x1, waiting for transfers between devices, body(): projected = lax.psum(local_terms, ('row', 'col'))  219 us
    dot_general x1, matrix products, body(): lax.dot_general(row_block, lax.all_gather(masked, 'row', axis=0, tiled=Tr...  10.4 us
  transfers between devices with their start and end apart: 3, of which 1 were waited for; matrix products, arithmetic and copies ran while one was open for 1% of the time, Pallas kernels for 0%

commit v1 on v0

--- a/solution.py
+++ b/solution.py
@@ -22,7 +22,7 @@
     local_terms = lax.dot_general(
         masked, vectors, (((0,), (0,)), ((), ())), preferred_element_type=jnp.float32
     )
-    projected = lax.psum(local_terms, ("row", "col"))
+    projected = jnp.sum(lax.all_gather(local_terms, ("row", "col")), axis=0)
     coupled = jnp.dot(
         weighted.astype(jnp.float32),
         projected,

time: 255 us -> 347 us (1.36)
  waiting for transfers between devices: 220 us -> 287 us
  local copies, waits for them, and re-layouts: 0.11 us -> 21.9 us
  other arithmetic: 3.27 us -> 9.22 us
    psum x1 -> x0, waiting for transfers between devices: 219 us -> none  [body(): projected = lax.psum(local_terms, ('row', 'col'))]
    all_gather x0 -> x1, waiting for transfers between devices: none -> 145 us  [body(): projected = jnp.sum(lax.all_gather(local_terms, ('row', 'col')), axis=0)]
    all_gather x1, waiting for transfers between devices: 0.01 us -> 111 us  [body(): lax.all_gather(masked, 'row', axis=0, tiled=True)]
    all_gather x1, waiting for transfers between devices: 0.01 us -> 30.4 us  [body(): row_block = lax.all_gather(weighted, 'col', axis=0, tiled=True)]
    unnamed x8 -> x7, local copies, waits for them, and re-layouts: 0.02 us -> 21.8 us
    reduce_sum x0 -> x1, other arithmetic: none -> 5.7 us  [body(): projected = jnp.sum(lax.all_gather(local_terms, ('row', 'col')), axis=0)]
  transfers between devices with their start and end apart: 3 -> 3, of which waited for: 1 -> 3; matrix products, arithmetic and copies ran while one was open for 1% -> 4% of each run, Pallas kernels for 0% -> 0%
where the time goes in v1:
time: 347 us; the launch traced here: 346 us
  waiting for transfers between devices  287 us (83%)
  local copies, waits for them, and re-layouts  21.9 us (6%)
  matrix products  14.4 us (4%)
  between operations  13.8 us (4%)
  other arithmetic  9.22 us (3%)
    all_gather x1, waiting for transfers between devices, body(): projected = jnp.sum(lax.all_gather(local_terms, ('row', 'col')), axis=0)  145 us
    all_gather x1, waiting for transfers between devices, body(): lax.all_gather(masked, 'row', axis=0, tiled=True)  111 us
    all_gather x1, waiting for transfers between devices, body(): row_block = lax.all_gather(weighted, 'col', axis=0, tiled=True)  30.4 us
    unnamed x7, local copies, waits for them, and re-layouts  21.8 us
    dot_general x1, matrix products, body(): lax.dot_general(row_block, lax.all_gather(masked, 'row', axis=0, tiled=Tr...  10.4 us
  transfers between devices with their start and end apart: 3, of which 3 were waited for; matrix products, arithmetic and copies ran while one was open for 4% of the time, Pallas kernels for 0%

profile of v1, /device:TPU:0, one launch (start us, length us, event | category | flops | bytes accessed | tf_op | source)
XLA Modules:
  0.0 346.3 jit_solution(9271300876347314312)
XLA Ops:
  7.2 0.0 copy-start.1
  7.2 0.0 copy-start.2
  7.2 0.0 all-gather.5.cloned.1.call-start
  7.2 0.7 iota_compare_fusion
  8.0 0.1 lt.18
  8.1 2.8 multiply_convert_fusion
  10.8 0.0 all-gather.5.cloned.1.call-update
  10.9 0.0 all-gather.7.cloned.1.call-start
  10.9 0.7 all-gather.7.cloned.1.call-update
  11.6 0.0 all-gather.9.cloned.1.call-start
  11.7 0.0 copy-done.1
  11.7 2.4 fusion.1
  14.0 0.0 all-gather.9.cloned.1.call-update
  14.1 0.0 copy-done.2
  14.1 30.4 %all-gather.5.cloned.1.call-done = bf16[576,3072]{1,0:T(8,128)(2,1)} async-done(((bf16[144,3072]{1,0:T(8,128)(2,1)}), bf16[576,3072]{1,0:T(8,128)(2,1)}) %all-gather.5.cloned.1.call-update) | async-done | bytes 3538960 | tf_op jit(solution)/shard_map/all_gather | solution.py:15
  44.5 111.1 %all-gather.7.cloned.1.call-done = bf16[1152,3072]{1,0:T(8,128)(2,1)} async-done(((bf16[144,3072]{1,0:T(8,128)(2,1)}), bf16[1152,3072]{1,0:T(8,128)(2,1)}) %all-gather.7.cloned.1.call-update) | async-done | bytes 7077904 | tf_op jit(solution)/shard_map/all_gather | solution.py:18
  155.6 10.4 %fusion = f32[576,1152]{1,0:T(8,128)} fusion(bf16[576,3072]{1,0:T(8,128)(2,1)} %all-gather.5.cloned.1.call-done, bf16[1152,3072]{1,0:T(8,128)(2,1)} %all-gather.7.cloned.1.call-done), kind=kOutput, calls=%fused_computation.6 | convolution fusion | flops 4076863488 | bytes 13271040 | tf_op jit(solution)/shard_map/dot_general | solution.py:16
  165.9 144.8 %all-gather.9.cloned.1.call-done = f32[98304,64]{0,1:T(8,128)} async-done(((f32[3072,64]{0,1:T(8,128)}), f32[98304,64]{0,1:T(8,128)}) %all-gather.9.cloned.1.call-update) | async-done | bytes 25165840 | tf_op jit(solution)/shard_map/all_gather | solution.py:25
  310.7 21.8 %copy.7 = f32[8,8,32,3072]{3,2,1,0:T(8,128)S(1)} copy(f32[8,8,32,3072]{3,1,2,0:T(8,128)} %bitcast.11) | data formatting | bytes 50331648
  332.4 0.0 copy-start
  332.5 5.7 %bitcast_reduce_fusion = f32[3072,64]{0,1:T(8,128)S(1)} fusion(f32[8,8,32,3072]{3,2,1,0:T(8,128)S(1)} %copy.7), kind=kLoop, calls=%fused_computation | loop fusion | flops 6094848 | bytes 25952256 | tf_op jit(solution)/shard_map/reduce_sum | solution.py:25
  338.2 0.0 copy-done
  338.2 1.6 convolution_add_fusion
  (1 shorter events, 0.0 us)
Async XLA Ops:
  7.2 4.5 %copy-start.1 = (bf16[144,64]{0,1:T(8,128)(2,1)S(1)}, bf16[144,64]{0,1:T(8,128)(2,1)}, u32[]{:S(2)}) copy-start(bf16[144,64]{0,1:T(8,128)(2,1)} %param.9) | copy-start | bytes 55300
  7.2 6.9 %copy-start.2 = (f32[144]{0:T(256)S(1)}, f32[144]{0:T(256)}, u32[]{:S(2)}) copy-start(f32[144]{0:T(256)} %param.8) | copy-start | bytes 1732
  7.2 37.3 %all-gather.5.cloned.1.call-start = ((), (), s32[]{:S(2)}) async-start(), calls=%async_computation | async-start | bytes 4423680 | tf_op jit(solution)/shard_map/all_gather | solution.py:15
  10.9 144.7 %all-gather.7.cloned.1.call-start = ((), (), s32[]{:S(2)}) async-start(), calls=%async_computation.1 | async-start | bytes 7962624 | tf_op jit(solution)/shard_map/all_gather | solution.py:18
  11.6 299.1 %all-gather.9.cloned.1.call-start = ((), (), s32[]{:S(2)}) async-start(), calls=%async_computation.2 | async-start | bytes 25952256 | tf_op jit(solution)/shard_map/all_gather | solution.py:25
  332.4 5.7 %copy-start = (bf16[144,3072]{1,0:T(8,128)(2,1)S(1)}, bf16[144,3072]{1,0:T(8,128)(2,1)}, u32[]{:S(2)}) copy-start(bf16[144,3072]{1,0:T(8,128)(2,1)} %get-tuple-element.2) | copy-start | bytes 2654212
Sparse Core Ops, SparseCore 0:
  11.0 33.4 all-gather.4
  47.2 108.2 all-gather.6
  158.4 152.2 all-gather.8

commit v2 on v0

--- a/solution.py
+++ b/solution.py
@@ -22,7 +22,7 @@
     local_terms = lax.dot_general(
         masked, vectors, (((0,), (0,)), ((), ())), preferred_element_type=jnp.float32
     )
-    projected = lax.psum(local_terms, ("row", "col"))
+    projected = lax.psum(lax.psum(local_terms, "col"), "row")
     coupled = jnp.dot(
         weighted.astype(jnp.float32),
         projected,

time: 255 us -> 310 us (1.22)
  waiting for transfers between devices: 220 us -> 277 us
    all_gather x1, waiting for transfers between devices: 0.01 us -> 110 us  [body(): lax.all_gather(masked, 'row', axis=0, tiled=True)]
    psum x1 -> x2, waiting for transfers between devices: 219 us -> 137 us  [body(): projected = lax.psum(lax.psum(local_terms, 'col'), 'row')]
    all_gather x1, waiting for transfers between devices: 0.01 us -> 28.1 us  [body(): row_block = lax.all_gather(weighted, 'col', axis=0, tiled=True)]
  transfers between devices with their start and end apart: 3 -> 4, of which waited for: 1 -> 4; matrix products, arithmetic and copies ran while one was open for 1% -> 1% of each run, Pallas kernels for 0% -> 0%
where the time goes in v2:
time: 310 us
  waiting for transfers between devices  277 us (89%)
  matrix products  15.6 us (5%)
  between operations  13.8 us (4%)
  other arithmetic  3.17 us (1%)
    psum x2, waiting for transfers between devices, body(): projected = lax.psum(lax.psum(local_terms, 'col'), 'row')  137 us
    all_gather x1, waiting for transfers between devices, body(): lax.all_gather(masked, 'row', axis=0, tiled=True)  110 us
    all_gather x1, waiting for transfers between devices, body(): row_block = lax.all_gather(weighted, 'col', axis=0, tiled=True)  28.1 us
    dot_general x1, matrix products, body(): lax.dot_general(row_block, lax.all_gather(masked, 'row', axis=0, tiled=Tr...  10.4 us
  transfers between devices with their start and end apart: 4, of which 4 were waited for; matrix products, arithmetic and copies ran while one was open for 1% of the time, Pallas kernels for 0%

profile of v2, /device:TPU:0, one launch (start us, length us, event | category | flops | bytes accessed | tf_op | source)
XLA Modules:
  0.0 309.8 jit_solution(11321916880770020517)
XLA Ops:
  7.2 0.0 copy-start.2
  7.2 0.0 all-reduce.3.cloned.1.call-start
  7.2 0.7 iota_compare_fusion
  7.9 0.1 lt.18
  8.0 2.4 multiply_convert_fusion
  10.5 0.0 copy-start
  10.5 0.0 copy-done.2
  10.5 1.8 fusion.1
  12.3 0.0 copy-start.3
  12.3 0.0 copy-start.1
  12.3 0.0 all-reduce.3.cloned.1.call-update
  12.3 0.0 all-reduce.5.cloned.1.call-start
  12.4 45.7 %all-reduce.3.cloned.1.call-done = f32[3072,64]{1,0:T(8,128)} async-done(((f32[3072,64]{1,0:T(8,128)}), f32[3072,64]{1,0:T(8,128)}) %all-reduce.3.cloned.1.call-update) | async-done | bytes 786448 | tf_op jit(solution)/shard_map/psum | solution.py:25
  58.0 0.0 all-reduce.5.cloned.1.call-update
  58.1 0.0 copy-done
  58.1 0.0 all-gather.3.cloned.1.call-start
  58.1 0.7 all-gather.3.cloned.1.call-update
  58.8 0.0 all-gather.5.cloned.1.call-start
  58.9 0.5 all-gather.5.cloned.1.call-update
  59.4 0.0 copy-done.3
  59.4 91.5 %all-reduce.5.cloned.1.call-done = f32[3072,64]{1,0:T(8,128)} async-done(((f32[3072,64]{1,0:T(8,128)}), f32[3072,64]{1,0:T(8,128)}) %all-reduce.5.cloned.1.call-update) | async-done | bytes 786448 | tf_op jit(solution)/shard_map/psum | solution.py:25
  150.9 0.0 copy-done.1
  150.9 3.5 %convolution_add_fusion = f32[144,64]{0,1:T(8,128)} fusion(bf16[144,3072]{1,0:T(8,128)(2,1)S(1)} %copy-done.1, f32[3072,64]{1,0:T(8,128)} %all-reduce.5.cloned.1.call-done, bf16[144,64]{0,1:T(8,128)(2,1)S(1)} %copy-done.2, f32[144]{0:T(256)S(1)} %broadcast_select_fusion.1), kind=kOutput, calls=%fused_computation.1 | convolution fusion | flops 339766272 | bytes 1727040 | tf_op jit(solution)/shard_map/dot_general | solution.py:26
  154.4 28.1 %all-gather.3.cloned.1.call-done = bf16[576,3072]{1,0:T(8,128)(2,1)} async-done(((bf16[144,3072]{1,0:T(8,128)(2,1)}), bf16[576,3072]{1,0:T(8,128)(2,1)}) %all-gather.3.cloned.1.call-update) | async-done | bytes 3538960 | tf_op jit(solution)/shard_map/all_gather | solution.py:15
  182.5 110.4 %all-gather.5.cloned.1.call-done = bf16[1152,3072]{1,0:T(8,128)(2,1)} async-done(((bf16[144,3072]{1,0:T(8,128)(2,1)}), bf16[1152,3072]{1,0:T(8,128)(2,1)}) %all-gather.5.cloned.1.call-update) | async-done | bytes 7077904 | tf_op jit(solution)/shard_map/all_gather | solution.py:18
  292.9 10.4 %fusion = f32[576,1152]{1,0:T(8,128)} fusion(bf16[576,3072]{1,0:T(8,128)(2,1)} %all-gather.3.cloned.1.call-done, bf16[1152,3072]{1,0:T(8,128)(2,1)} %all-gather.5.cloned.1.call-done), kind=kOutput, calls=%fused_computation.5 | convolution fusion | flops 4076863488 | bytes 13271040 | tf_op jit(solution)/shard_map/dot_general | solution.py:16
  (1 shorter events, 0.0 us)
Async XLA Ops:
  7.2 3.3 %copy-start.2 = (bf16[144,64]{0,1:T(8,128)(2,1)S(1)}, bf16[144,64]{0,1:T(8,128)(2,1)}, u32[]{:S(2)}) copy-start(bf16[144,64]{0,1:T(8,128)(2,1)} %param.9) | copy-start | bytes 55300
  7.2 50.9 %all-reduce.3.cloned.1.call-start = ((), (), s32[]{:S(2)}) async-start(), calls=%async_computation.2 | async-start | bytes 3145728 | tf_op jit(solution)/shard_map/psum | solution.py:25
  10.5 47.6 %copy-start = (bf16[144,3072]{1,0:T(8,128)(2,1)}, bf16[144,3072]{1,0:T(8,128)(2,1)S(1)}, u32[]{:S(2)}) copy-start(bf16[144,3072]{1,0:T(8,128)(2,1)S(1)} %get-tuple-element.3) | copy-start | bytes 2654212
  12.3 47.1 %copy-start.3 = (f32[144]{0:T(256)S(1)}, f32[144]{0:T(256)}, u32[]{:S(2)}) copy-start(f32[144]{0:T(256)} %param.8) | copy-start | bytes 1732
  12.3 138.6 %copy-start.1 = (bf16[144,3072]{1,0:T(8,128)(2,1)S(1)}, bf16[144,3072]{1,0:T(8,128)(2,1)}, u32[]{:S(2)}) copy-start(bf16[144,3072]{1,0:T(8,128)(2,1)} %get-tuple-element.2) | copy-start | bytes 2654212
  12.3 138.6 %all-reduce.5.cloned.1.call-start = ((), (), s32[]{:S(2)}) async-start(), calls=%async_computation.3 | async-start | bytes 3145728 | tf_op jit(solution)/shard_map/psum | solution.py:25
  58.1 124.4 %all-gather.3.cloned.1.call-start = ((), (), s32[]{:S(2)}) async-start(), calls=%async_computation | async-start | bytes 4423680 | tf_op jit(solution)/shard_map/all_gather | solution.py:15
  58.8 234.1 %all-gather.5.cloned.1.call-start = ((), (), s32[]{:S(2)}) async-start(), calls=%async_computation.1 | async-start | bytes 7962624 | tf_op jit(solution)/shard_map/all_gather | solution.py:18
Sparse Core Ops, SparseCore 0:
  12.4 45.5 all-reduce.2
  61.6 89.3 all-reduce.4
  152.5 29.9 all-gather.2
  184.6 108.2 all-gather.4
